TPU v7x, 32 devices: a whole 2x2x4 slice. The times are simulated.
32 devices in a mesh: section: 16 (over z, y, x), tensor: 2 (over core).
Axes of the slice: x: 2, y: 2, z: 4, core: 2. Of those that a mesh axis runs over, the one named last changes fastest.
Arguments:
- hidden_in: bfloat16 [128, 8192], P(None, 'tensor'), may hold values from -36 to 36
- segment_ids: int32 [4, 32], replicated, may hold values from 0 to 7, never falling along the last dimension, each value on 1 to 8 neighbouring positions
- segment_job: int32 [4, 8], replicated, may hold values from 0 to 5
- job_adapter: int32 [6], replicated, may hold values from 0 to 3
- owner: int32 [16], P('section'), may hold values from 0 to 1
- frozen: bfloat16 [16, 8192, 4096], P('section', None, 'tensor'), may hold values from -0.0625 to 0.0625
- norm_gain: bfloat16 [16, 4096], P('section'), may hold values from 0.3984375 to 1.59375
- inbox_down: bfloat16 [16, 2, 4096, 128], P('section', 'tensor'), may hold values from -0.0625 to 0.0625
- inbox_up: bfloat16 [16, 2, 128, 4096], P('section', 'tensor'), may hold values from -1 to 1
Outputs:
- section_out: bfloat16 [16, 128, 4096], P('section', None, 'tensor')
Inputs may be any that keep to these rules, and one draw needn't show every extreme that they name: `segment_ids`: within each micro-batch the segment numbers never fall, and each of the 8 segments has 1 to 8 tokens.
All inputs are finite; a program needn't handle non-finite values.
Results may differ from a plain program's by a relative error of at most 0.02.
Values may be sent and summed in bfloat16 or wider, within the bound.
A program may use at most 128 MiB of HBM per device.

v0:
```python
import functools
import jax
import jax.numpy as jnp
from jax import lax
from jax.experimental import pallas as pl
from jax.experimental.pallas import tpu as pltpu
from jax.sharding import PartitionSpec as P

R = 32
MESH = pl.DeviceIdType.MESH
epsilon = 1e-05


def kernel(
    sections, tensors, units, rows, piece, chunks, ranks, jobs_of,
    hidden, ids, seg_job, job_ad, owner, frozen, gain, idown, iup,
    out,
    w, xbuf, xg, acc, outbuf, gother, dbuf, ubuf, dsel, usel, lowbuf, kept, square, scale,
    wsem, vsem, xsem, psem, fsend, osend, hsem, dsem, usem, isend, gsem, lsem, lsend,
):
    levels = sections // 2
    step = piece // chunks
    full = 2 * tensors * piece
    segs, jobs = jobs_of
    s = lax.axis_index("section")
    t = lax.axis_index("tensor")
    h = lax.rem(s, 2)
    level = s // 2
    other = s + 1 - 2 * h
    b = 2 * t + h

    def peer(d):
        return lax.rem(t + d, tensors)

    def cols(c):
        return pl.ds(pl.multiple_of(c * step, step), step)

    def part(k):
        return pl.ds(pl.multiple_of(k * piece, piece), piece)

    def near_rows(hh, c):
        return pl.ds(pl.multiple_of((2 * t + hh) * piece + c * step, step), step)

    def far_rows(d):
        return pl.ds(pl.multiple_of(2 * peer(d) * piece, piece), 2 * piece)

    def near_weight(hh, c):
        return pltpu.make_async_copy(frozen.at[0, near_rows(hh, c), :], w.at[near_rows(hh, c), :], wsem.at[hh, c])

    def far_weight(d, c):
        return pltpu.make_async_copy(
            frozen.at[0, far_rows(d), cols(c)], w.at[far_rows(d), cols(c)], vsem.at[d, c]
        )

    def remote(src, dst, send, recv, section, tensor):
        return pltpu.make_async_remote_copy(
            src_ref=src, dst_ref=dst, send_sem=send, recv_sem=recv,
            device_id=(section, tensor), device_id_type=MESH,
        )

    def landed(ref, sem):
        pltpu.make_async_copy(ref, ref, sem).wait()

    own_down = pltpu.make_async_copy(idown.at[0, 0, part(t), :], dbuf.at[t], dsem.at[t])
    own_up = pltpu.make_async_copy(iup.at[0, 0, :, part(t)], ubuf.at[t], usem.at[t])

    @pl.when(level == 0)
    def _():
        for hh in range(2):
            for c in range(chunks):
                def read(m, _, hh=hh, c=c):
                    slot = pl.ds(c * step, step)
                    pltpu.make_async_copy(
                        hidden.at[pl.ds(pl.multiple_of(m * rows, rows), rows), pl.ds(hh * piece + c * step, step)],
                        xbuf.at[m, 2 * t + hh, :, slot],
                        xsem.at[m, hh, c],
                    ).start()
                    return 0
                lax.fori_loop(0, units, read, 0)
    own_down.start()
    own_up.start()
    for c in range(chunks):
        for hh in range(2):
            near_weight(hh, c).start()
    for c in range(chunks):
        for d in range(1, tensors):
            far_weight(d, c).start()

    barrier = pltpu.get_barrier_semaphore()

    def greet(section, tensor):
        pl.semaphore_signal(barrier, inc=1, device_id=(section, tensor), device_id_type=MESH)

    for d in range(1, tensors):
        greet(s, peer(d))
    for d in range(tensors):
        greet(other, peer(d))

    @pl.when(level > 0)
    def _():
        greet(s - 2, t)
        greet(other - 2, t)

    @pl.when(level < levels - 1)
    def _():
        greet(s + 2, t)
        greet(other + 2, t)

    ends = (level > 0).astype(jnp.int32) + (level < levels - 1).astype(jnp.int32)
    pl.semaphore_wait(barrier, 2 * tensors - 1 + 2 * ends)

    def send_down(d):
        return remote(idown.at[0, 0, part(peer(d)), :], dbuf.at[t], isend.at[0, d], dsem.at[t], s, peer(d))

    def send_up(d):
        return remote(iup.at[0, 0, :, part(peer(d))], ubuf.at[t], isend.at[1, d], usem.at[t], s, peer(d))

    send_gain = remote(gain, gother, gsem.at[0], gsem.at[1], other, t)
    send_gain.start()
    for d in range(1, tensors):
        send_down(d).start()
        send_up(d).start()

    def forward(m, c, hh, d):
        ref = xbuf.at[m, 2 * t + hh, :, cols(c)]
        return remote(ref, ref, fsend.at[m, d, hh, c], psem.at[m, t, hh, c], s, peer(d))

    def forward_one(m, c, hh):
        landed(xbuf.at[m, 2 * t + hh, :, cols(c)], xsem.at[m, hh, c])
        for d in range(1, tensors):
            forward(m, c, hh, d).start()

    def low_to(m, side, d):
        ref = lowbuf.at[m, b]
        section = s if side == 0 else other
        return remote(ref, ref, lsend.at[m, side, d], lsem.at[m, b], section, peer(d))

    def low_part(m):
        own = xbuf[m, b].astype(jnp.float32) * gain[0:1, part(t)].astype(jnp.float32)
        lowbuf[m, b] = jnp.dot(own.astype(jnp.bfloat16), dsel[...], preferred_element_type=jnp.float32)
        for side in range(2):
            for d in range(1 - side, tensors):
                low_to(m, side, d).start()

    def send_out(m, c, side):
        section = (s if side == 0 else other) + 2
        return remote(
            outbuf.at[m, :, cols(c)], xbuf.at[m, b, :, cols(c)],
            osend.at[m, side, c], xsem.at[m, h, c], section, t,
        )

    def write_out(m):
        return pltpu.make_async_copy(
            outbuf.at[m], out.at[0, pl.ds(pl.multiple_of(m * rows, rows), rows), :], hsem.at[m]
        )

    def forward_chunk(m, c):
        forward_one(m, c, h)

        @pl.when(c == chunks - 1)
        def _():
            low_part(m)

        forward_one(m, c, 1 - h)

    def gained(x, k_side, where_gain):
        near = gain[0:1, where_gain].astype(jnp.float32)
        far = gother[0:1, where_gain].astype(jnp.float32)
        return (x * jnp.where(h == k_side, near, far)).astype(jnp.bfloat16)

    own_down.wait()
    own_up.wait()
    for d in range(1, tensors):
        landed(dbuf.at[peer(d)], dsem.at[peer(d)])
        landed(ubuf.at[peer(d)], usem.at[peer(d)])
    who = owner[0]
    down, up = dbuf[0], ubuf[0]
    for k in range(1, tensors):
        down = jnp.where(who == k, dbuf[k], down)
        up = jnp.where(who == k, ubuf[k], up)
    dsel[...] = down
    usel[...] = up
    send_gain.wait_recv()

    def unit(m, _):
        square[...] = jnp.zeros_like(square)
        acc[...] = jnp.zeros_like(acc)
        forward_chunk(m, 0)

        def near(c, _):
            @pl.when(c + 1 < chunks)
            def _():
                forward_chunk(m, c + 1)

            @pl.when(m == 0)
            def _():
                for hh in range(2):
                    near_weight(hh, c).wait()

            part_sum = acc[...]
            total = jnp.zeros((rows, 1), jnp.float32)
            for hh in range(2):
                x = xbuf[m, 2 * t + hh, :, cols(c)].astype(jnp.float32)
                total += jnp.sum(x * x, axis=1, keepdims=True)
                values = gained(x, hh, pl.ds(pl.multiple_of(t * piece + c * step, step), step))
                part_sum += jnp.dot(values, w[near_rows(hh, c), :], preferred_element_type=jnp.float32)
            acc[...] = part_sum
            square[...] += jnp.broadcast_to(total, square.shape)
            return 0

        lax.fori_loop(0, chunks, near, 0)

        total = square[:, 0:1]
        for d in range(1, tensors):
            for hh in range(2):
                for c in range(chunks):
                    landed(xbuf.at[m, 2 * peer(d) + hh, :, pl.ds(c * step, step)], psem.at[m, peer(d), hh, c])
                x = xbuf[m, 2 * peer(d) + hh].astype(jnp.float32)
                total += jnp.sum(x * x, axis=1, keepdims=True)
                xg[d - 1, :, hh * piece : (hh + 1) * piece] = gained(x, hh, part(peer(d)))
        scale[...] = jnp.broadcast_to(lax.rsqrt(total / full + epsilon), scale.shape)

        def chunk(c, _):
            @pl.when(m == 0)
            def _():
                for d in range(1, tensors):
                    far_weight(d, c).wait()

            main = acc[:, cols(c)]
            for d in range(1, tensors):
                main += jnp.dot(xg[d - 1], w[far_rows(d), cols(c)], preferred_element_type=jnp.float32)

            @pl.when(c == 0)
            def _():
                for side in range(2):
                    for d in range(1 - side, tensors):
                        blk = 2 * peer(d) + (h if side == 0 else 1 - h)
                        landed(lowbuf.at[m, blk], lsem.at[m, blk])
                low = lowbuf[m, 0]
                for k in range(1, 2 * tensors):
                    low = low + lowbuf[m, k]
                low = low * scale[:, 0:1]
                seg = ids[pl.ds(m, 1), :]
                slot = jnp.zeros_like(seg)
                for g in range(segs):
                    slot = jnp.where(seg == g, job_ad[seg_job[m, g]], slot)
                column = lax.broadcasted_iota(jnp.int32, (ranks, rows), 0) // R
                hit = jnp.where(column == slot, 1.0, 0.0).astype(jnp.bfloat16)
                eye = jnp.where(
                    lax.broadcasted_iota(jnp.int32, (rows, rows), 0)
                    == lax.broadcasted_iota(jnp.int32, (rows, rows), 1), 1.0, 0.0
                ).astype(jnp.bfloat16)
                mask = lax.dot_general(eye, hit, (((1,), (1,)), ((), ())), preferred_element_type=jnp.float32)
                kept[...] = jnp.where(mask > 0.5, low, 0.0).astype(jnp.bfloat16)

            adapted = jnp.dot(kept[...], usel[:, cols(c)], preferred_element_type=jnp.float32)
            fresh = xbuf[m, b, :, cols(c)].astype(jnp.float32) + main * scale[:, 0:1] + adapted
            outbuf[m, :, cols(c)] = fresh.astype(jnp.bfloat16)

            @pl.when(level < levels - 1)
            def _():
                for side in range(2):
                    send_out(m, c, side).start()
            return 0

        lax.fori_loop(0, chunks, chunk, 0)
        write_out(m).start()
        return 0

    lax.fori_loop(0, units, unit, 0)

    send_gain.wait_send()
    for d in range(1, tensors):
        send_down(d).wait_send()
        send_up(d).wait_send()

    def drain(m, _):
        for d in range(1, tensors):
            for hh in range(2):
                for c in range(chunks):
                    forward(m, c, hh, d).wait_send()
        for side in range(2):
            for d in range(1 - side, tensors):
                low_to(m, side, d).wait_send()

        @pl.when(level < levels - 1)
        def _():
            for side in range(2):
                for c in range(chunks):
                    send_out(m, c, side).wait_send()
        write_out(m).wait()
        return 0

    lax.fori_loop(0, units, drain, 0)


def local(
    hidden_in, segment_ids, segment_job, job_adapter, owner, frozen, norm_gain, inbox_down, inbox_up
):
    tensors = lax.axis_size("tensor")
    sections = lax.axis_size("section")
    units, rows = segment_ids.shape
    depth, piece = frozen.shape[1:]
    ranks = inbox_down.shape[3]
    chunks = max(1, min(2, piece // 256))
    step = piece // chunks
    bf16, f32 = jnp.bfloat16, jnp.float32
    anywhere = pl.BlockSpec(memory_space=pl.ANY)
    smem = pl.BlockSpec(memory_space=pltpu.SMEM)
    vmem = pl.BlockSpec(memory_space=pltpu.VMEM)
    dma = pltpu.SemaphoreType.DMA
    body = functools.partial(
        kernel, sections, tensors, units, rows, piece, chunks, ranks,
        (segment_job.shape[1], job_adapter.shape[0]),
    )
    return pl.pallas_call(
        body,
        out_shape=jax.ShapeDtypeStruct((1, units * rows, piece), bf16),
        in_specs=[anywhere, vmem, smem, smem, smem, anywhere, vmem, anywhere, anywhere],
        out_specs=anywhere,
        scratch_shapes=[
            pltpu.VMEM((depth, piece), bf16),
            pltpu.VMEM((units, 2 * tensors, rows, piece), bf16),
            pltpu.VMEM((max(1, tensors - 1), rows, 2 * piece), bf16),
            pltpu.VMEM((rows, piece), f32),
            pltpu.VMEM((units, rows, piece), bf16),
            pltpu.VMEM(norm_gain.shape, bf16),
            pltpu.VMEM((tensors, piece, ranks), bf16),
            pltpu.VMEM((tensors, ranks, piece), bf16),
            pltpu.VMEM((piece, ranks), bf16),
            pltpu.VMEM((ranks, piece), bf16),
            pltpu.VMEM((units, 2 * tensors, rows, ranks), f32),
            pltpu.VMEM((rows, ranks), bf16),
            pltpu.VMEM((rows, 128), f32),
            pltpu.VMEM((rows, 128), f32),
            dma((2, chunks)),
            dma((tensors, chunks)),
            dma((units, 2, chunks)),
            dma((units, tensors, 2, chunks)),
            dma((units, tensors, 2, chunks)),
            dma((units, 2, chunks)),
            dma((units,)),
            dma((tensors,)),
            dma((tensors,)),
            dma((2, tensors)),
            dma((2,)),
            dma((units, 2 * tensors)),
            dma((units, 2, tensors)),
        ],
        compiler_params=pltpu.CompilerParams(
            collective_id=0, has_side_effects=True, vmem_limit_bytes=60 * 2**20
        ),
    )(hidden_in, segment_ids, segment_job, job_adapter, owner, frozen, norm_gain, inbox_down, inbox_up)


def solution(mesh):
    return jax.shard_map(
        local,
        mesh=mesh,
        in_specs=(
            P(None, "tensor"),
            P(),
            P(),
            P(),
            P("section"),
            P("section", None, "tensor"),
            P("section", None),
            P("section", "tensor", None, None),
            P("section", "tensor", None, None),
        ),
        out_specs=P("section", None, "tensor"),
        check_vma=False,
    )
```

profile of v0, /device:TPU:29, one launch (start us, length us, event | category | flops | bytes accessed | tf_op | source)
XLA Modules:
  0.0 130.9 jit_solution(9186270179354619111)
XLA Ops:
  0.7 128.3 %shard_map.91 = bf16[1,128,2048]{2,1,0:T(8,128)(2,1)} custom-call(bf16[128,4096]{1,0:T(8,128)(2,1)} %hidden.1, s32[4,32]{1,0:T(4,128)} %ids.1, s32[4,8]{1,0:T(4,128)} %seg_job.1, s32[6]{0:T(128)} %job_ad.1, s32[1]{0:T(128)S(6)} %copy.11.owner, bf16[1,8192,2048]{2,1,0:T(8,128)(2,1)} %frozen.1, bf16[1,4096]{1,0:T(2,128)(2,1)} %gain.1, ...), custom_call_target="tpu_custom_call" | custom-call | tf_op jit(solution)/shard_map/pallas_call | solution.py:316
  129.0 1.9 %copy.12 = bf16[1,128,2048]{2,1,0:T(8,128)(2,1)} copy(bf16[1,128,2048]{2,1,0:T(8,128)(2,1)} %shard_map.91) | data formatting | bytes 1048576
where the time goes:
time: 132 us; the launch traced here: 131 us
  Pallas kernels  128 us (97%)
  local copies, waits for them, and re-layouts  1.88 us (1%)
    pallas_call x1, Pallas kernels, local(): pl.pallas_call(body, out_shape=jax.ShapeDtypeStruct((1, units * rows, pie...  128 us

commit v1 on v0

v1 whole, which is shorter than its diff:
```python
import functools
import jax
import jax.numpy as jnp
from jax import lax
from jax.experimental import pallas as pl
from jax.experimental.pallas import tpu as pltpu
from jax.sharding import PartitionSpec as P

R = 32
TILE = 256
MESH = pl.DeviceIdType.MESH
epsilon = 1e-05
f32, bf16 = jnp.float32, jnp.bfloat16


def run(steps):
    products = [step for step in steps if isinstance(step, list)]

    def push(n):
        if n < len(products):
            for q, (rhs, _, _) in enumerate(products[n]):
                pltpu.matmul_push_rhs(rhs(), staging_register=n % 2, mxu_index=q)

    push(0)
    push(1)
    n = 0
    for step in steps:
        if isinstance(step, list):
            for _, acc, lhs in step:
                pltpu.matmul_acc_lhs(acc, lhs(), load_staged_rhs=n % 2)
            push(n + 2)
            n += 1
        else:
            step()


def kernel(
    sections, tensors, units, rows, piece, chunks, quarters, ranks, jobs_of,
    hidden, ids, seg_job, job_ad, owner, frozen, gain, idown, iup,
    out,
    w, x0, xg0, xbuf, outbuf, gother, dbuf, ubuf, dsel, usel, lowbuf, mask, kept0,
    wsem, hidsem, hidsend, dsem, usem, isend, gsem, ysem, xsem, psem, lsem,
    osend, xsend, fsend, lsend, wout,
):
    levels = sections // 2
    step = piece // chunks
    tokens = units * rows
    full = 2 * tensors * piece
    depth = full // quarters
    inner = step // TILE
    tiles = piece // TILE
    segs, jobs = jobs_of
    s = lax.axis_index("section")
    t = lax.axis_index("tensor")
    h = lax.rem(s, 2)
    level = s // 2
    other = s + 1 - 2 * h
    b = 2 * t + h
    last = level == levels - 1

    def peer(d):
        return lax.rem(t + d, tensors)

    def at(start, size):
        return pl.ds(pl.multiple_of(start, TILE), size)

    def part(k):
        return at(k * piece, piece)

    def remote(src, dst, send, recv, section, tensor):
        return pltpu.make_async_remote_copy(
            src_ref=src, dst_ref=dst, send_sem=send, recv_sem=recv,
            device_id=(section, tensor), device_id_type=MESH,
        )

    def landed(ref, sem):
        pltpu.make_async_copy(ref, ref, sem).wait()

    def unit_rows(m):
        return pl.ds(pl.multiple_of(m * rows, rows), rows)

    own_hidden = pltpu.make_async_copy(hidden, x0.at[t], hidsem.at[t])
    own_down = pltpu.make_async_copy(idown.at[0, 0, part(t), :], dbuf.at[t], dsem.at[t])
    own_up = pltpu.make_async_copy(iup.at[0, 0, :, part(t)], ubuf.at[t], usem.at[t])

    def weight_cols(j, k):
        here = (at(k * depth, depth), at(j * step, step))
        return pltpu.make_async_copy(frozen.at[(0,) + here], w.at[here], wsem.at[j, k])

    def weight_rows(j, k):
        share = depth // chunks
        here = at((k * chunks + j) * share, share)
        return pltpu.make_async_copy(frozen.at[0, here, :], w.at[here, :], wsem.at[j, k])

    @pl.when(level == 0)
    def _():
        own_hidden.start()

    own_down.start()
    own_up.start()

    @pl.when(level == 0)
    def _():
        for j in range(chunks):
            for k in range(quarters):
                weight_cols(j, k).start()

    @pl.when(level > 0)
    def _():
        for j in range(chunks):
            for k in range(quarters):
                weight_rows(j, k).start()

    barrier = pltpu.get_barrier_semaphore()

    def greet(section, tensor):
        pl.semaphore_signal(barrier, inc=1, device_id=(section, tensor), device_id_type=MESH)

    for d in range(1, tensors):
        greet(s, peer(d))
    for d in range(tensors):
        greet(other, peer(d))

    @pl.when(level > 0)
    def _():
        greet(s - 2, t)

    @pl.when(level < levels - 1)
    def _():
        greet(s + 2, t)

    ends = (level > 0).astype(jnp.int32) + (level < levels - 1).astype(jnp.int32)
    pl.semaphore_wait(barrier, 2 * tensors - 1 + ends)

    def send_hidden(d):
        return remote(hidden, x0.at[t], hidsend.at[d], hidsem.at[t], s, peer(d))

    def send_down(d):
        return remote(idown.at[0, 0, part(peer(d)), :], dbuf.at[t], isend.at[0, d], dsem.at[t], s, peer(d))

    def send_up(d):
        return remote(iup.at[0, 0, :, part(peer(d))], ubuf.at[t], isend.at[1, d], usem.at[t], s, peer(d))

    send_gain = remote(gain, gother, gsem.at[0], gsem.at[1], other, t)
    send_gain.start()

    @pl.when(level == 0)
    def _():
        for d in range(1, tensors):
            send_hidden(d).start()

    for d in range(1, tensors):
        send_down(d).start()
        send_up(d).start()

    def send_out(m, c):
        return remote(outbuf.at[m, c], xbuf.at[m, b, c], osend.at[m], ysem.at[m, c], s + 2, t)

    def write_out(m, c):
        return pltpu.make_async_copy(outbuf.at[m, c], out.at[0, unit_rows(m), at(c * step, step)], wout.at[m])

    def low_sends(slot, ref):
        for side in range(2):
            for d in range(1 - side, tensors):
                remote(ref, ref, lsend.at[slot], lsem.at[slot, b], s if side == 0 else other, peer(d)).start()

    def low_blocks():
        return [2 * peer(d) + (h if side == 0 else 1 - h) for side in range(2) for d in range(1 - side, tensors)]

    for m in range(units):
        seg = ids[pl.ds(m, 1), :]
        slot = jnp.zeros_like(seg)
        for g in range(segs):
            slot = jnp.where(seg == g, job_ad[seg_job[m, g]], slot)
        eye = lax.broadcasted_iota(jnp.int32, (rows, rows), 0) == lax.broadcasted_iota(jnp.int32, (rows, rows), 1)
        spread = jnp.where(eye, jnp.broadcast_to(slot.astype(f32), (rows, rows)), 0.0)
        column = jnp.sum(spread, axis=1, keepdims=True)
        rank = lax.broadcasted_iota(jnp.int32, (rows, ranks), 1) // R
        mask[m * rows : (m + 1) * rows, :] = jnp.where(rank.astype(f32) == column, 1.0, 0.0)
    dsel[...] = jnp.zeros_like(dsel)
    usel[...] = jnp.zeros_like(usel)
    own_down.wait()
    own_up.wait()
    for d in range(1, tensors):
        landed(dbuf.at[peer(d)], dsem.at[peer(d)])
        landed(ubuf.at[peer(d)], usem.at[peer(d)])
    who = owner[0]
    down, up = dbuf[0], ubuf[0]
    for k in range(1, tensors):
        down = jnp.where(who == k, dbuf[k], down)
        up = jnp.where(who == k, ubuf[k], up)
    dsel[:, 0:ranks] = down
    usel[0:ranks, :] = up
    send_gain.wait_recv()

    def widen(kept):
        return jnp.concatenate([kept, jnp.zeros((kept.shape[0], TILE - ranks), bf16)], axis=1)

    def first(accs):
        own_hidden.wait()
        for d in range(1, tensors):
            landed(x0.at[peer(d)], hidsem.at[peer(d)])
        square = jnp.zeros((tokens, 128), f32)
        for k in range(tensors):
            for hh in range(2):
                def prepare(i, square, k=k, hh=hh):
                    x = x0[k, :, at(hh * piece + i * TILE, TILE)].astype(f32)
                    where_gain = at(k * piece + i * TILE, TILE)
                    g = jnp.where(h == hh, gain[0:1, where_gain].astype(f32), gother[0:1, where_gain].astype(f32))
                    xg0[(2 * k + hh) * tiles + i] = (x * g).astype(bf16)
                    for v in range(TILE // 128):
                        y = x[:, v * 128 : (v + 1) * 128]
                        square = square + y * y
                    return square
                square = lax.fori_loop(0, tiles, prepare, square)
        scale = lax.rsqrt(jnp.sum(square, axis=1, keepdims=True) / full + epsilon)

        steps = []
        for i in range(0, tiles, 2):
            steps.append([
                (
                    lambda i=i, q=q: dsel[(i + q) * TILE : (i + q + 1) * TILE, :],
                    accs[0][q],
                    lambda i=i, q=q: xg0[b * tiles + i + q],
                )
                for q in range(2)
            ])
        run(steps)
        low = pltpu.matmul_pop(accs[0][0]) + pltpu.matmul_pop(accs[0][1])
        lowbuf[b] = low[:, 0:ranks]
        low_sends(0, lowbuf.at[b])

        def main(j):
            def quarter(k, _):
                weight_cols(j, k).wait()
                deep = depth // TILE
                steps = []
                for i in range(deep):
                    steps.append([
                        (
                            lambda i=i, q=q: w[at(k * depth + i * TILE, TILE), j * step + q * TILE : j * step + (q + 1) * TILE],
                            accs[j][q],
                            lambda i=i: xg0[k * deep + i],
                        )
                        for q in range(2)
                    ])
                run(steps)
                return 0
            lax.fori_loop(0, quarters, quarter, 0)

        def finish(j):
            run([[
                (
                    lambda q=q: usel[:, j * step + q * TILE : j * step + (q + 1) * TILE],
                    accs[j][q],
                    lambda: kept0[...],
                )
                for q in range(2)
            ]])
            for q in range(2):
                old = x0[t, :, at(h * piece + j * step + q * TILE, TILE)].astype(f32)
                fresh = (old + pltpu.matmul_pop(accs[j][q]) * scale).astype(bf16)
                for m in range(units):
                    outbuf[m, j, :, q * TILE : (q + 1) * TILE] = fresh[m * rows : (m + 1) * rows]

            @pl.when(jnp.logical_not(last))
            def _():
                for m in range(min(2, units)):
                    send_out(m, j).start()
            for m in range(units):
                write_out(m, j).start()

        early = min(2, chunks)
        for j in range(early):
            main(j)
        for blk in low_blocks():
            landed(lowbuf.at[blk], lsem.at[0, blk])
        low = lowbuf[0]
        for k in range(1, 2 * tensors):
            low = low + lowbuf[k]
        kept0[...] = widen((low * mask[...]).astype(bf16))
        for j in range(early):
            finish(j)
        for j in range(early, chunks):
            main(j)
            finish(j)

        @pl.when(jnp.logical_not(last))
        def _():
            for m in range(2, units):
                for j in range(chunks):
                    send_out(m, j).start()

    arrivals = sorted(
        [(c, 0, c) for c in range(chunks)]
        + [(c + 1.4, 1, c) for c in range(chunks)]
        + [(c + 3.4, 2, c) for c in range(chunks)]
        + [(c + 4.8, 3, c) for c in range(chunks)]
    )

    def later(accs, lows):
        for j in range(chunks):
            for k in range(quarters):
                weight_rows(j, k).wait()

        def unit(m, _):
            here = {"square": jnp.zeros((rows, 128), f32)}
            steps = []

            def pieces(kind):
                hh = h if kind < 2 else 1 - h
                gains = gain if kind < 2 else gother
                if kind % 2 == 0:
                    return [(t, 2 * t + hh, gains)]
                return [(peer(d), 2 * peer(d) + hh, gains) for d in range(1, tensors)]

            def arrive(kind, c, owner_of, blk):
                if kind == 0:
                    landed(xbuf.at[m, blk, c], ysem.at[m, c])
                    remote(xbuf.at[m, blk, c], xbuf.at[m, blk, c], xsend.at[m], xsem.at[m, c], other, t).start()
                elif kind == 2:
                    landed(xbuf.at[m, blk, c], xsem.at[m, c])
                else:
                    landed(xbuf.at[m, blk, c], psem.at[m, owner_of, kind // 2, c])
                if kind % 2 == 0:
                    for d in range(1, tensors):
                        remote(
                            xbuf.at[m, blk, c], xbuf.at[m, blk, c],
                            fsend.at[m], psem.at[m, t, kind // 2, c], s, peer(d),
                        ).start()

            def prepare(c, owner_of, blk, gains):
                x = xbuf[m, blk, c].astype(f32)
                g = gains[0:1, at(owner_of * piece + c * step, step)].astype(f32)
                here["x"] = (x * g).astype(bf16)
                for v in range(step // 128):
                    y = x[:, v * 128 : (v + 1) * 128]
                    here["square"] = here["square"] + y * y

            def lhs(i):
                return lambda: here["x"][:, i * TILE : (i + 1) * TILE]

            def product(blk, c, i, j):
                return [
                    (
                        lambda q=q: w[
                            at(blk * piece + c * step + i * TILE, TILE),
                            j * step + q * TILE : j * step + (q + 1) * TILE,
                        ],
                        accs[j][q],
                        lhs(i),
                    )
                    for q in range(2)
                ]

            def low_product(c, i):
                return [
                    (
                        lambda q=q: dsel[c * step + (i + q) * TILE : c * step + (i + q + 1) * TILE, :],
                        lows[q],
                        lhs(i + q),
                    )
                    for q in range(2)
                ]

            def low_out():
                low = pltpu.matmul_pop(lows[0]) + pltpu.matmul_pop(lows[1])
                lowbuf[b, unit_rows(m), :] = low[:, 0:ranks]
                low_sends(m, lowbuf.at[b, unit_rows(m)])

            def low_in():
                for blk in low_blocks():
                    landed(lowbuf.at[blk, unit_rows(m)], lsem.at[m, blk])
                low = lowbuf[0, unit_rows(m), :]
                for k in range(1, 2 * tensors):
                    low = low + lowbuf[k, unit_rows(m), :]
                here["kept"] = widen((low * mask[unit_rows(m), :]).astype(bf16))

            work = [(kind, c) + p for _, kind, c in arrivals for p in pieces(kind)]
            pending = False
            for kind, c, owner_of, blk, gains in work[:-1]:
                steps.append(lambda a=(kind, c, owner_of, blk): arrive(*a))
                steps.append(lambda a=(c, owner_of, blk, gains): prepare(*a))
                for i in range(inner):
                    for j in range(chunks):
                        steps.append(product(blk, c, i, j))
                if kind == 0:
                    for i in range(0, inner, 2):
                        steps.append(low_product(c, i))
                if pending:
                    steps.append(low_out)
                pending = kind == 0 and c == chunks - 1
            if pending:
                steps.append(low_out)

            kind, c, owner_of, blk, gains = work[-1]
            steps.append(low_in)
            steps.append(lambda: arrive(kind, c, owner_of, blk))
            steps.append(lambda: prepare(c, owner_of, blk, gains))

            def scaling():
                total = jnp.sum(here["square"], axis=1, keepdims=True)
                here["scale"] = lax.rsqrt(total / full + epsilon)

            def leave(j):
                for q in range(2):
                    cols = slice(q * TILE, (q + 1) * TILE)
                    old = xbuf[m, b, j, :, cols].astype(f32)
                    fresh = old + pltpu.matmul_pop(accs[j][q]) * here["scale"]
                    outbuf[m, j, :, cols] = fresh.astype(bf16)

                @pl.when(jnp.logical_not(last))
                def _():
                    send_out(m, j).start()
                write_out(m, j).start()

            for j in range(chunks):
                for i in range(inner):
                    steps.append(product(blk, c, i, j))
                steps.append([
                    (
                        lambda j=j, q=q: usel[:, j * step + q * TILE : j * step + (q + 1) * TILE],
                        accs[j][q],
                        lambda: here["kept"],
                    )
                    for q in range(2)
                ])
                if j == 0:
                    steps.append(scaling)
                if j > 0:
                    steps.append(lambda j=j: leave(j - 1))
            steps.append(lambda: leave(chunks - 1))
            run(steps)
            return 0

        lax.fori_loop(0, units, unit, 0)

        for m in range(units):
            landed(xbuf.at[m, 0], xsend.at[m])
            if tensors > 1:
                landed(xbuf.at[m, 0 : 2 * (tensors - 1)], fsend.at[m])
            landed(lowbuf.at[0 : 2 * tensors - 1, m * rows : (m + 1) * rows], lsend.at[m])

    def body(*flat):
        for acc in flat:
            pltpu.matmul_pop(acc)
        wide = [flat[2 * j : 2 * j + 2] for j in range(chunks)]
        narrow = [flat[2 * (chunks + j) : 2 * (chunks + j) + 2] for j in range(chunks)]
        lows = flat[4 * chunks :]

        @pl.when(level == 0)
        def _():
            first(wide)

        @pl.when(level > 0)
        def _():
            later(narrow, lows)

    def acc(q, height):
        return pltpu.ACC(q)((height, TILE), f32)

    pl.run_scoped(
        body,
        *[acc(q, tokens) for _ in range(chunks) for q in range(2)],
        *[acc(q, rows) for _ in range(chunks) for q in range(2)],
        *[acc(q, rows) for q in range(2)],
    )

    send_gain.wait_send()
    for d in range(1, tensors):
        send_down(d).wait_send()
        send_up(d).wait_send()

    @pl.when(level == 0)
    def _():
        for d in range(1, tensors):
            send_hidden(d).wait_send()
        landed(lowbuf.at[0 : 2 * tensors - 1], lsend.at[0])

    @pl.when(jnp.logical_not(last))
    def _():
        for m in range(units):
            landed(outbuf.at[m], osend.at[m])

    for m in range(units):
        landed(outbuf.at[m], wout.at[m])


def local(
    hidden_in, segment_ids, segment_job, job_adapter, owner, frozen, norm_gain, inbox_down, inbox_up
):
    tensors = lax.axis_size("tensor")
    sections = lax.axis_size("section")
    units, rows = segment_ids.shape
    depth, piece = frozen.shape[1:]
    ranks = inbox_down.shape[3]
    step = 2 * TILE
    chunks = piece // step
    quarters = 4
    tokens = units * rows
    anywhere = pl.BlockSpec(memory_space=pl.ANY)
    smem = pl.BlockSpec(memory_space=pltpu.SMEM)
    vmem = pl.BlockSpec(memory_space=pltpu.VMEM)
    dma = pltpu.SemaphoreType.DMA
    body = functools.partial(
        kernel, sections, tensors, units, rows, piece, chunks, quarters, ranks,
        (segment_job.shape[1], job_adapter.shape[0]),
    )
    return pl.pallas_call(
        body,
        out_shape=jax.ShapeDtypeStruct((1, tokens, piece), bf16),
        in_specs=[anywhere, vmem, smem, smem, smem, anywhere, vmem, anywhere, anywhere],
        out_specs=anywhere,
        scratch_shapes=[
            pltpu.VMEM((depth, piece), bf16),
            pltpu.VMEM((tensors, tokens, 2 * piece), bf16),
            pltpu.VMEM((depth // TILE, tokens, TILE), bf16),
            pltpu.VMEM((units, 2 * tensors, chunks, rows, step), bf16),
            pltpu.VMEM((units, chunks, rows, step), bf16),
            pltpu.VMEM(norm_gain.shape, bf16),
            pltpu.VMEM((tensors, piece, ranks), bf16),
            pltpu.VMEM((tensors, ranks, piece), bf16),
            pltpu.VMEM((piece, TILE), bf16),
            pltpu.VMEM((TILE, piece), bf16),
            pltpu.VMEM((2 * tensors, tokens, ranks), f32),
            pltpu.VMEM((tokens, ranks), f32),
            pltpu.VMEM((tokens, TILE), bf16),
            dma((chunks, quarters)),
            dma((tensors,)),
            dma((tensors,)),
            dma((tensors,)),
            dma((tensors,)),
            dma((2, tensors)),
            dma((2,)),
            dma((units, chunks)),
            dma((units, chunks)),
            dma((units, tensors, 2, chunks)),
            dma((units, 2 * tensors)),
            dma((units,)),
            dma((units,)),
            dma((units,)),
            dma((units,)),
            dma((units,)),
        ],
        compiler_params=pltpu.CompilerParams(
            collective_id=0, has_side_effects=True, vmem_limit_bytes=60 * 2**20
        ),
    )(hidden_in, segment_ids, segment_job, job_adapter, owner, frozen, norm_gain, inbox_down, inbox_up)


def solution(mesh):
    mapped = jax.shard_map(
        local,
        mesh=mesh,
        in_specs=(
            P(None, "tensor"),
            P(),
            P(),
            P(),
            P("section"),
            P("section", None, "tensor"),
            P("section", None),
            P("section", "tensor", None, None),
            P("section", "tensor", None, None),
        ),
        out_specs=P("section", None, "tensor"),
        check_vma=False,
    )
    return mapped
```

time: 132 us -> 113 us (0.86)
  Pallas kernels: 128 us -> 110 us
    pallas_call x1, Pallas kernels: 128 us -> 110 us  [local(): pl.pallas_call(body, out_shape=jax.ShapeDtypeStruct((1, tokens, piece), b...]
where the time goes in v1:
time: 113 us
  Pallas kernels  110 us (97%)
  local copies, waits for them, and re-layouts  1.88 us (2%)
    pallas_call x1, Pallas kernels, local(): pl.pallas_call(body, out_shape=jax.ShapeDtypeStruct((1, tokens, piece), b...  110 us

profile of v1, /device:TPU:29, one launch (start us, length us, event | category | flops | bytes accessed | tf_op | source)
XLA Modules:
  0.0 112.7 jit_solution(5457149859743263385)
XLA Ops:
  0.7 110.2 %shard_map.91 = bf16[1,128,2048]{2,1,0:T(8,128)(2,1)} custom-call(bf16[128,4096]{1,0:T(8,128)(2,1)} %hidden.1, s32[4,32]{1,0:T(4,128)} %ids.1, s32[4,8]{1,0:T(4,128)} %seg_job.1, s32[6]{0:T(128)} %job_ad.1, s32[1]{0:T(128)S(6)} %copy.11.owner, bf16[1,8192,2048]{2,1,0:T(8,128)(2,1)} %frozen.1, bf16[1,4096]{1,0:T(2,128)(2,1)} %gain.1, ...), custom_call_target="tpu_custom_call" | custom-call | tf_op jit(solution)/shard_map/pallas_call | solution.py:509
  110.8 1.9 %copy.12 = bf16[1,128,2048]{2,1,0:T(8,128)(2,1)} copy(bf16[1,128,2048]{2,1,0:T(8,128)(2,1)} %shard_map.91) | data formatting | bytes 1048576

commit v2 on v1

v2 whole, which is shorter than its diff:
```python
import functools
import jax
import jax.numpy as jnp
from jax import lax
from jax.experimental import pallas as pl
from jax.experimental.pallas import tpu as pltpu
from jax.sharding import PartitionSpec as P

R = 32
TILE = 256
UNIT = 32
DIRECT = 0
EARLY = 0
TAIL = 2
LAG = 4
MESH = pl.DeviceIdType.MESH
epsilon = 1e-05
f32, bf16 = jnp.float32, jnp.bfloat16


def products_of(steps):
    return [step for step in steps if isinstance(step, list)]


def stage(product, n):
    for q, (rhs, _, _) in enumerate(product):
        pltpu.matmul_push_rhs(rhs(), staging_register=n % 2, mxu_index=q)


def run(steps, carried=False):
    products = products_of(steps)
    count = len(products)
    if not carried:
        for n in range(min(2, count)):
            stage(products[n], n)
    n = 0
    for step in steps:
        if isinstance(step, list):
            for _, acc, lhs in step:
                pltpu.matmul_acc_lhs(acc, lhs(), load_staged_rhs=n % 2)
            if n + 2 < count:
                stage(products[n + 2], n)
            elif carried:
                stage(products[n + 2 - count], n)
            n += 1
        else:
            with jax.named_scope(getattr(step, "label", "step")):
                step()


def kernel(
    sections, tensors, batches, rows, piece, chunks, ranks, jobs_of,
    hidden, ids, seg_job, job_ad, owner, frozen, gain, idown, iup,
    out,
    w, x0, xg0, xbuf, outbuf, gother, dout, uout, dbuf, ubuf, dsel, usel, lowbuf, mask, kept0, sq0,
    wsem, hidsem, hidsend, ready, dsem, usem, isend, gsem, ysem, xsem, psem, lsem,
    osend, xsend, fsend, lsend, wout,
):
    levels = sections // 2
    step = piece // chunks
    batch, spread = batches
    tokens = batch * spread
    units = -(-tokens // rows)
    short = tokens - (units - 1) * rows
    full = 2 * tensors * piece
    blocks = 2 * tensors
    inner = step // TILE
    tiles = piece // TILE
    segs, jobs = jobs_of
    window = 6
    direct = min(DIRECT, chunks - 1)
    early = min(EARLY, chunks - 1)
    s = lax.axis_index("section")
    t = lax.axis_index("tensor")
    h = lax.rem(s, 2)
    level = s // 2
    other = s + 1 - 2 * h
    b = 2 * t + h
    last = level == levels - 1

    def peer(d):
        return lax.rem(t + d, tensors)

    def at(start, size):
        return pl.ds(pl.multiple_of(start, TILE), size)

    def part(k):
        return at(k * piece, piece)

    def remote(src, dst, send, recv, section, tensor):
        return pltpu.make_async_remote_copy(
            src_ref=src, dst_ref=dst, send_sem=send, recv_sem=recv,
            device_id=(section, tensor), device_id_type=MESH,
        )

    def landed(ref, sem):
        pltpu.make_async_copy(ref, ref, sem).wait()

    def unit_rows(m):
        return pl.ds(pl.multiple_of(m * rows, 8), rows)

    own_hidden = pltpu.make_async_copy(hidden, x0.at[t], hidsem.at[t])
    own_down = pltpu.make_async_copy(idown.at[0, 0, part(t), :], dbuf.at[t], dsem.at[t])
    own_up = pltpu.make_async_copy(iup.at[0, 0, :, part(t)], ubuf.at[t], usem.at[t])

    def read_down(d):
        return pltpu.make_async_copy(idown.at[0, 0, part(peer(d)), :], dout.at[d], ready.at[0, d])

    def read_up(d):
        return pltpu.make_async_copy(iup.at[0, 0, :, part(peer(d))], uout.at[d], ready.at[1, d])

    def weight_cols(j, blk):
        here = (part(blk), at(j * step, step))
        return pltpu.make_async_copy(frozen.at[(0,) + here], w.at[here], wsem.at[j, blk])

    def weight_rows(j, blk):
        here = at(blk * piece + j * step, step)
        return pltpu.make_async_copy(frozen.at[0, here, :], w.at[here, :], wsem.at[j, blk])

    def rest():
        return [2 * t + 1 - h] + [2 * peer(d) + hh for d in range(1, tensors) for hh in range(2)]

    barrier = pltpu.get_barrier_semaphore()

    def greet(section, tensor):
        pl.semaphore_signal(barrier, inc=1, device_id=(section, tensor), device_id_type=MESH)

    for d in range(1, tensors):
        greet(s, peer(d))
    for d in range(tensors):
        greet(other, peer(d))

    @pl.when(level > 0)
    def _():
        greet(s - 2, t)
        greet(other - 2, t)

    @pl.when(level < levels - 1)
    def _():
        greet(s + 2, t)
        greet(other + 2, t)

    @pl.when(level == 0)
    def _():
        own_hidden.start()

    def read_adapters():
        own_down.start()
        own_up.start()

    for d in range(1, tensors):
        read_down(d).start()
        read_up(d).start()

    fetches = [(j, b) for j in range(chunks)] + [(j, blk) for j in range(chunks) for blk in rest()]

    def fetch(n):
        if n < len(fetches):
            weight_cols(*fetches[n]).start()

    def fetched(n):
        weight_cols(*fetches[n]).wait()
        fetch(n + window)

    @pl.when(level == 0)
    def _():
        fetch(0)

    @pl.when(level > 0)
    def _():
        read_adapters()
        for j in range(chunks):
            for blk in range(blocks):
                weight_rows(j, blk).start()

    def gain_row(hh, start, size):
        near = gain[0:1, at(start, size)].astype(f32)
        return near if hh is None else jnp.where(h == hh, near, gother[0:1, at(start, size)].astype(f32))

    def prepare_first(owner_of, hh, square):
        blk = 2 * owner_of + (h if hh is None else hh)
        start = (h if hh is None else hh) * piece

        def one(i, square):
            x = x0[owner_of, :, at(start + i * TILE, TILE)].astype(f32)
            xg0[blk * tiles + i] = (x * gain_row(hh, owner_of * piece + i * TILE, TILE)).astype(bf16)
            for v in range(TILE // 128):
                y = x[:, v * 128 : (v + 1) * 128]
                square = square + y * y
            return square

        return lax.fori_loop(0, tiles, one, square)

    @pl.when(level == 0)
    def _():
        own_hidden.wait()
        for n in range(1, 3):
            fetch(n)
        read_adapters()
        for n in range(3, window):
            fetch(n)
        sq0[...] = prepare_first(t, None, jnp.zeros((tokens, 128), f32))

    ends = (level > 0).astype(jnp.int32) + (level < levels - 1).astype(jnp.int32)
    with jax.named_scope("barrier"):
        pl.semaphore_wait(barrier, 2 * tensors - 1 + 2 * ends)

    def send_hidden(d):
        return remote(x0.at[t], x0.at[t], hidsend.at[d], hidsem.at[t], s, peer(d))

    def send_down(d):
        return remote(dout.at[d], dbuf.at[t], isend.at[0, d], dsem.at[t], s, peer(d))

    def send_up(d):
        return remote(uout.at[d], ubuf.at[t], isend.at[1, d], usem.at[t], s, peer(d))

    send_gain = remote(gain, gother, gsem.at[0], gsem.at[1], other, t)
    send_gain.start()

    @pl.when(level == 0)
    def _():
        for d in range(1, tensors):
            send_hidden(d).start()

    for d in range(1, tensors):
        read_down(d).wait()
        send_down(d).start()
        read_up(d).wait()
        send_up(d).start()

    def send_out(m, c):
        return remote(outbuf.at[m, c], xbuf.at[m, b, c], osend.at[m], ysem.at[m, c], s + 2, t)

    def send_across(m, c):
        return remote(outbuf.at[m, c], xbuf.at[m, b, c], osend.at[m], xsem.at[m, c], other + 2, t)

    def send_both(m, c):
        send_out(m, c).start()
        if c >= chunks - direct:
            send_across(m, c).start()

    def sent(m):
        landed(outbuf.at[m], osend.at[m])
        if direct:
            landed(outbuf.at[m, 0:direct], osend.at[m])

    def write_out(m, c):
        def write(size):
            here = pl.ds(pl.multiple_of(m * rows, 8), size)
            pltpu.make_async_copy(
                outbuf.at[m, c, 0:size], out.at[0, here, at(c * step, step)], wout.at[m]
            ).start()

        if short == rows:
            write(rows)
        elif isinstance(m, int):
            write(short if m == units - 1 else rows)
        else:
            pl.when(m < units - 1)(lambda: write(rows))
            pl.when(m == units - 1)(lambda: write(short))

    def low_sends(slot, ref):
        for side in range(2):
            for d in range(1 - side, tensors):
                remote(ref, ref, lsend.at[slot], lsem.at[slot, b], s if side == 0 else other, peer(d)).start()

    def low_blocks():
        return [2 * peer(d) + (h if side == 0 else 1 - h) for side in range(2) for d in range(1 - side, tensors)]

    for m in range(batch):
        seg = ids[pl.ds(m, 1), :]
        slot = jnp.zeros_like(seg)
        for g in range(segs):
            slot = jnp.where(seg == g, job_ad[seg_job[m, g]], slot)
        square_of = (spread, spread)
        eye = lax.broadcasted_iota(jnp.int32, square_of, 0) == lax.broadcasted_iota(jnp.int32, square_of, 1)
        lanes = jnp.where(eye, jnp.broadcast_to(slot.astype(f32), square_of), 0.0)
        column = jnp.sum(lanes, axis=1, keepdims=True)
        rank = lax.broadcasted_iota(jnp.int32, (spread, ranks), 1) // R
        mask[m * spread : (m + 1) * spread, :] = jnp.where(rank.astype(f32) == column, 1.0, 0.0)
    if short < rows:
        mask[tokens:, :] = jnp.zeros((units * rows - tokens, ranks), f32)

    def adapters():
        own_down.wait()
        own_up.wait()
        for d in range(1, tensors):
            landed(dbuf.at[peer(d)], dsem.at[peer(d)])
            landed(ubuf.at[peer(d)], usem.at[peer(d)])
        who = owner[0]
        down, up = dbuf[0], ubuf[0]
        for k in range(1, tensors):
            down = jnp.where(who == k, dbuf[k], down)
            up = jnp.where(who == k, ubuf[k], up)
        dsel[:, 0:ranks] = down
        dsel[:, ranks:] = jnp.zeros((piece, TILE - ranks), bf16)
        usel[0:ranks, :] = up
        usel[ranks:, :] = jnp.zeros((TILE - ranks, piece), bf16)

    def widen(kept):
        return jnp.concatenate([kept, jnp.zeros((kept.shape[0], TILE - ranks), kept.dtype)], axis=1)

    def first(accs, lows):
        def main(j, begin, end):
            steps = []
            for n, (_, blk) in enumerate(fetches[begin:end]):
                wait = lambda n=n: fetched(begin + n)
                wait.label = "wwait"
                if n == 0:
                    wait()
                else:
                    steps.insert(n * tiles - 2 + n - 1, wait)
                for i in range(tiles):
                    steps.append([
                        (
                            lambda i=i, q=q, blk=blk: w[
                                at(blk * piece + i * TILE, TILE), j * step + q * TILE : j * step + (q + 1) * TILE
                            ],
                            accs[j][q],
                            lambda i=i, blk=blk: xg0[blk * tiles + i],
                        )
                        for q in range(2)
                    ])
            run(steps)

        for j in range(chunks):
            main(j, j, j + 1)
        with jax.named_scope("gainwait"):
            send_gain.wait_recv()
        square = prepare_first(t, 1 - h, sq0[...])
        for d in range(1, tensors):
            with jax.named_scope("hidwait"):
                landed(x0.at[peer(d)], hidsem.at[peer(d)])
            for hh in range(2):
                square = prepare_first(peer(d), hh, square)
        scale = lax.rsqrt(jnp.sum(square, axis=1, keepdims=True) / full + epsilon)

        with jax.named_scope("adapters"):
            adapters()
        steps = []
        for i in range(0, tiles, 2):
            steps.append([
                (
                    lambda i=i, q=q: dsel[(i + q) * TILE : (i + q + 1) * TILE, :],
                    lows[q],
                    lambda i=i, q=q: xg0[b * tiles + i + q],
                )
                for q in range(2)
            ])
        run(steps)
        low = pltpu.matmul_pop(lows[0]) + pltpu.matmul_pop(lows[1])
        lowbuf[b, 0:tokens] = low[:, 0:ranks]
        low_sends(0, lowbuf.at[b, 0:tokens])

        def finish(j):
            run([[
                (
                    lambda q=q: usel[:, j * step + q * TILE : j * step + (q + 1) * TILE],
                    accs[j][q],
                    lambda: kept0[...],
                )
                for q in range(2)
            ]])
            for q in range(2):
              with jax.named_scope('fin'):
                old = x0[t, :, at(h * piece + j * step + q * TILE, TILE)].astype(f32)
                fresh = old + pltpu.matmul_pop(accs[j][q]) * scale
                for m in range(units):
                    size = short if m == units - 1 else rows
                    cols = slice(q * TILE, (q + 1) * TILE)
                    outbuf[m, j, 0:size, cols] = fresh[m * rows : m * rows + size].astype(bf16)
                    if size < rows:
                        outbuf[m, j, size:, cols] = jnp.zeros((rows - size, TILE), bf16)

            @pl.when(jnp.logical_not(last))
            def _():
                send_both(0, j)
            for m in range(units):
                write_out(m, j)

        ready_chunks = min(2, chunks)
        for j in range(ready_chunks):
            main(j, chunks + j * len(rest()), chunks + (j + 1) * len(rest()))
        with jax.named_scope("lowwait"):
            for blk in low_blocks():
                landed(lowbuf.at[blk, 0:tokens], lsem.at[0, blk])
        low = lowbuf[0, 0:tokens]
        for k in range(1, 2 * tensors):
            low = low + lowbuf[k, 0:tokens]
        kept0[...] = widen((low * mask[0:tokens]).astype(bf16))
        for j in range(ready_chunks):
            finish(j)
        for j in range(ready_chunks, chunks):
            main(j, chunks + j * len(rest()), chunks + (j + 1) * len(rest()))
            finish(j)

        @pl.when(jnp.logical_not(last))
        def _():
            for m in range(1, units):
                sent(m - 1)
                for j in range(chunks):
                    send_both(m, j)
            sent(units - 1)

    crossing = list(range(chunks - direct, chunks))
    relayed = list(range(chunks - direct))
    arrivals = [(0, kind, c) for kind in range(2) for c in range(chunks)]
    late = relayed[:1] + crossing + relayed[1:]
    arrivals += [(0, kind, c) for kind in range(2, 4) for c in late]
    lead = min(3, inner * chunks - 1)

    def label(name, step):
        step.label = name
        return step

    def later(accs, lows):
        adapters()
        send_gain.wait_recv()
        with jax.named_scope("wrow"):
            for j in range(chunks):
                for blk in range(blocks):
                    weight_rows(j, blk).wait()

        def pieces(kind):
            hh = h if kind < 2 else 1 - h
            gains = gain if kind < 2 else gother
            if kind % 2 == 0:
                return [(t, 2 * t + hh, gains)]
            return [(peer(d), 2 * peer(d) + hh, gains) for d in range(1, tensors)]

        work = [(kind, c) + p for _, kind, c in arrivals for p in pieces(kind)]

        def arrive(m, kind, c, owner_of, blk):
            ref = xbuf.at[m, blk, c]
            if kind == 0:
                landed(ref, ysem.at[m, c])
                if c < chunks - direct:
                    remote(ref, ref, xsend.at[m], xsem.at[m, c], other, t).start()
            elif kind == 2:
                landed(ref, xsem.at[m, c])
            else:
                landed(ref, psem.at[m, owner_of, kind // 2, c])
            if kind % 2 == 0:
                for d in range(1, tensors):
                    remote(ref, ref, fsend.at[m], psem.at[m, t, kind // 2, c], s, peer(d)).start()

        def unit_steps(m):
            here = {"square": jnp.zeros((rows, 128), f32)}
            steps = []

            def prepare(key):
                _, c, owner_of, blk, gains = work[key]
                x = xbuf[m, blk, c].astype(f32)
                here[key] = x * gains[0:1, at(owner_of * piece + c * step, step)].astype(f32)
                for v in range(step // 128):
                    y = x[:, v * 128 : (v + 1) * 128]
                    here["square"] = here["square"] + y * y

            def lhs(key, i):
                return lambda: here[key][:, i * TILE : (i + 1) * TILE]

            def product(key, i, j):
                _, c, _, blk, _ = work[key]
                return [
                    (
                        lambda q=q: w[
                            at(blk * piece + c * step + i * TILE, TILE),
                            j * step + q * TILE : j * step + (q + 1) * TILE,
                        ],
                        accs[j][q],
                        lhs(key, i),
                    )
                    for q in range(2)
                ]

            def low_product(key, i):
                start = work[key][1] * step + i * TILE
                return [
                    (
                        lambda q=q: dsel[start + q * TILE : start + (q + 1) * TILE, :],
                        lows[q],
                        lhs(key, i + q),
                    )
                    for q in range(2)
                ]

            def low_out():
                low = pltpu.matmul_pop(lows[0]) + pltpu.matmul_pop(lows[1])
                lowbuf[b, unit_rows(m), :] = low[:, 0:ranks]
                low_sends(m, lowbuf.at[b, unit_rows(m)])

            def low_in():
                for blk in low_blocks():
                    landed(lowbuf.at[blk, unit_rows(m)], lsem.at[m, blk])
                low = lowbuf[0, unit_rows(m), :]
                for k in range(1, 2 * tensors):
                    low = low + lowbuf[k, unit_rows(m), :]
                here["kept"] = widen(low * mask[unit_rows(m), :])

            def meet(key):
                kind, c, owner_of, blk, _ = work[key]
                found = [lambda: prepare(key)]
                if kind > 0 or c >= early:
                    name = "arr" + "YDXE"[kind] + str(c)
                    found = [label(name, lambda: arrive(m, kind, c, owner_of, blk))] + found
                return found

            def scaling():
                total = jnp.sum(here["square"], axis=1, keepdims=True)
                here["scale"] = lax.rsqrt(total / full + epsilon)

            def leave(j):
                for q in range(2):
                    cols = slice(q * TILE, (q + 1) * TILE)
                    old = xbuf[m, b, j, :, cols].astype(f32)
                    fresh = old + pltpu.matmul_pop(accs[j][q]) * here["scale"]
                    outbuf[m, j, :, cols] = fresh.astype(bf16)

                @pl.when(jnp.logical_not(last))
                def _():
                    send_both(m, j)
                write_out(m, j)
                if j < early:
                    @pl.when(m + 1 < units)
                    def _():
                        arrive(m + 1, 0, j, t, b)

            pending = False
            steps += meet(0)
            tail = len(work) - TAIL
            for key, (kind, c, _, _, _) in enumerate(work[:tail]):
                low_out_at = len(steps) + inner * chunks // 2
                for i in range(inner):
                    for j in range(chunks):
                        steps.append(product(key, i, j))
                if kind == 0:
                    for i in range(0, inner, 2):
                        steps.append(low_product(key, i))
                if pending:
                    steps.insert(low_out_at, label("lowout", low_out))
                pending = kind == 0 and c == chunks - 1
                ahead = meet(key + 1)
                if key + 1 == tail:
                    ahead = [label("lowin", low_in)] + ahead
                    for more in range(tail + 1, len(work)):
                        ahead += meet(more)
                steps[len(steps) - lead : len(steps) - lead] = ahead
            if pending:
                steps.append(low_out)
            for j in range(chunks):
                for key in range(tail, len(work)):
                    for i in range(inner):
                        steps.append(product(key, i, j))
                steps.append([
                    (
                        lambda j=j, q=q: usel[:, j * step + q * TILE : j * step + (q + 1) * TILE],
                        accs[j][q],
                        lambda: here["kept"],
                    )
                    for q in range(2)
                ])
                if j == 0:
                    steps.append(scaling)
                if j > 0:
                    back = len(steps) - max(0, len(products_of(steps[-TAIL * inner - 1 :])) - LAG)
                    steps.insert(back, label("leave", lambda j=j: leave(j - 1)))
            steps.append(label("leave", lambda: leave(chunks - 1)))
            return steps

        begin = products_of(unit_steps(0))
        carried = len(begin) % 2 == 0
        if carried:
            for n in range(2):
                stage(begin[n], n)
        for c in range(early):
            with jax.named_scope("first"):
                arrive(0, 0, c, t, b)

        def unit(m, _):
            run(unit_steps(m), carried)
            return 0

        lax.fori_loop(0, units, unit, 0)
        if carried:
            for n in range(2):
                for q in range(2):
                    pltpu.matmul_acc_lhs(accs[0][q], jnp.zeros((rows, TILE), f32), load_staged_rhs=n)
            for q in range(2):
                pltpu.matmul_pop(accs[0][q])

        for m in range(units):
            if chunks > direct:
                landed(xbuf.at[m, 0, 0 : chunks - direct], xsend.at[m])
            if tensors > 1:
                landed(xbuf.at[m, 0 : 2 * (tensors - 1)], fsend.at[m])
            landed(lowbuf.at[0 : 2 * tensors - 1, m * rows : (m + 1) * rows], lsend.at[m])

    def body(*flat):
        for acc in flat:
            pltpu.matmul_pop(acc)
        pairs = [flat[2 * j : 2 * j + 2] for j in range(2 * chunks + 2)]

        @pl.when(level == 0)
        def _():
            first(pairs[:chunks], pairs[-2])

        @pl.when(level > 0)
        def _():
            later(pairs[chunks:-2], pairs[-1])

    heights = chunks * [tokens] + chunks * [rows] + [tokens, rows]
    pl.run_scoped(body, *[pltpu.ACC(q)((height, TILE), f32) for height in heights for q in range(2)])

    send_gain.wait_send()
    for d in range(1, tensors):
        send_down(d).wait_send()
        send_up(d).wait_send()

    @pl.when(level == 0)
    def _():
        for d in range(1, tensors):
            send_hidden(d).wait_send()
        landed(lowbuf.at[0 : 2 * tensors - 1, 0:tokens], lsend.at[0])

    @pl.when(jnp.logical_not(last) & (level > 0))
    def _():
        for m in range(units):
            sent(m)

    for m in range(units):
        landed(outbuf.at[m, :, 0 : short if m == units - 1 else rows], wout.at[m])


def local(
    hidden_in, segment_ids, segment_job, job_adapter, owner, frozen, norm_gain, inbox_down, inbox_up
):
    tensors = lax.axis_size("tensor")
    sections = lax.axis_size("section")
    batches = segment_ids.shape
    depth, piece = frozen.shape[1:]
    ranks = inbox_down.shape[3]
    step = 2 * TILE
    chunks = piece // step
    tokens = batches[0] * batches[1]
    rows = min(UNIT, tokens)
    units = -(-tokens // rows)
    anywhere = pl.BlockSpec(memory_space=pl.ANY)
    smem = pl.BlockSpec(memory_space=pltpu.SMEM)
    vmem = pl.BlockSpec(memory_space=pltpu.VMEM)
    dma = pltpu.SemaphoreType.DMA
    body = functools.partial(
        kernel, sections, tensors, batches, rows, piece, chunks, ranks,
        (segment_job.shape[1], job_adapter.shape[0]),
    )
    return pl.pallas_call(
        body,
        out_shape=jax.ShapeDtypeStruct((1, tokens, piece), bf16),
        in_specs=[anywhere, vmem, smem, smem, smem, anywhere, vmem, anywhere, anywhere],
        out_specs=anywhere,
        scratch_shapes=[
            pltpu.VMEM((depth, piece), bf16),
            pltpu.VMEM((tensors, tokens, 2 * piece), bf16),
            pltpu.VMEM((depth // TILE, tokens, TILE), bf16),
            pltpu.VMEM((units, 2 * tensors, chunks, rows, step), bf16),
            pltpu.VMEM((units, chunks, rows, step), bf16),
            pltpu.VMEM(norm_gain.shape, bf16),
            pltpu.VMEM((tensors, piece, ranks), bf16),
            pltpu.VMEM((tensors, ranks, piece), bf16),
            pltpu.VMEM((tensors, piece, ranks), bf16),
            pltpu.VMEM((tensors, ranks, piece), bf16),
            pltpu.VMEM((piece, TILE), bf16),
            pltpu.VMEM((TILE, piece), bf16),
            pltpu.VMEM((2 * tensors, units * rows, ranks), f32),
            pltpu.VMEM((units * rows, ranks), f32),
            pltpu.VMEM((tokens, TILE), bf16),
            pltpu.VMEM((tokens, 128), f32),
            dma((chunks, 2 * tensors)),
            dma((tensors,)),
            dma((tensors,)),
            dma((2, tensors)),
            dma((tensors,)),
            dma((tensors,)),
            dma((2, tensors)),
            dma((2,)),
            dma((units, chunks)),
            dma((units, chunks)),
            dma((units, tensors, 2, chunks)),
            dma((units, 2 * tensors)),
            dma((units,)),
            dma((units,)),
            dma((units,)),
            dma((units,)),
            dma((units,)),
        ],
        compiler_params=pltpu.CompilerParams(
            collective_id=0, has_side_effects=True, vmem_limit_bytes=60 * 2**20
        ),
    )(hidden_in, segment_ids, segment_job, job_adapter, owner, frozen, norm_gain, inbox_down, inbox_up)


def solution(mesh):
    mapped = jax.shard_map(
        local,
        mesh=mesh,
        in_specs=(
            P(None, "tensor"),
            P(),
            P(),
            P(),
            P("section"),
            P("section", None, "tensor"),
            P("section", None),
            P("section", "tensor", None, None),
            P("section", "tensor", None, None),
        ),
        out_specs=P("section", None, "tensor"),
        check_vma=False,
    )
    return mapped
```

time: 113 us -> 106 us (0.938)
  Pallas kernels: 110 us -> 104 us
    pallas_call x1, Pallas kernels: 110 us -> 104 us  [local(): pl.pallas_call(body, out_shape=jax.ShapeDtypeStruct((1, tokens, piece), b...]
where the time goes in v2:
time: 106 us
  Pallas kernels  104 us (98%)
  local copies, waits for them, and re-layouts  1.88 us (2%)
    pallas_call x1, Pallas kernels, local(): pl.pallas_call(body, out_shape=jax.ShapeDtypeStruct((1, tokens, piece), b...  104 us

profile of v2, /device:TPU:29, one launch (start us, length us, event | category | flops | bytes accessed | tf_op | source)
XLA Modules:
  0.0 106.3 jit_solution(2393584791123545599)
XLA Ops:
  0.7 103.7 %shard_map.91 = bf16[1,128,2048]{2,1,0:T(8,128)(2,1)} custom-call(bf16[128,4096]{1,0:T(8,128)(2,1)} %hidden.1, s32[4,32]{1,0:T(4,128)} %ids.1, s32[4,8]{1,0:T(4,128)} %seg_job.1, s32[6]{0:T(128)} %job_ad.1, s32[1]{0:T(128)S(6)} %copy.11.owner, bf16[1,8192,2048]{2,1,0:T(8,128)(2,1)} %frozen.1, bf16[1,4096]{1,0:T(2,128)(2,1)} %gain.1, ...), custom_call_target="tpu_custom_call" | custom-call | tf_op jit(solution)/shard_map/pallas_call | solution.py:655
  104.4 1.9 %copy.12 = bf16[1,128,2048]{2,1,0:T(8,128)(2,1)} copy(bf16[1,128,2048]{2,1,0:T(8,128)(2,1)} %shard_map.91) | data formatting | bytes 1048576

commit v3 on v2

--- a/solution.py
+++ b/solution.py
@@ -11,7 +11,8 @@
 UNIT = 32
 DIRECT = 0
 EARLY = 0
-TAIL = 2
+DELAYS = (0, 4, 8, 12)
+TAIL = 1
 LAG = 4
 MESH = pl.DeviceIdType.MESH
 epsilon = 1e-05
@@ -378,7 +379,7 @@
             for m in range(units):
                 write_out(m, j)
 
-        ready_chunks = min(2, chunks)
+        ready_chunks = min(3, chunks)
         for j in range(ready_chunks):
             main(j, chunks + j * len(rest()), chunks + (j + 1) * len(rest()))
         with jax.named_scope("lowwait"):
@@ -402,11 +403,7 @@
                     send_both(m, j)
             sent(units - 1)
 
-    crossing = list(range(chunks - direct, chunks))
-    relayed = list(range(chunks - direct))
-    arrivals = [(0, kind, c) for kind in range(2) for c in range(chunks)]
-    late = relayed[:1] + crossing + relayed[1:]
-    arrivals += [(0, kind, c) for kind in range(2, 4) for c in late]
+    arrivals = sorted((c + delay, kind, c) for kind, delay in enumerate(DELAYS) for c in range(chunks))
     lead = min(3, inner * chunks - 1)
 
     def label(name, step):

time: 106 us -> 105 us (level)
  Pallas kernels: 104 us -> 102 us
    pallas_call x1, Pallas kernels: 104 us -> 102 us  [local(): pl.pallas_call(body, out_shape=jax.ShapeDtypeStruct((1, tokens, piece), b...]
where the time goes in v3:
time: 105 us; the launch traced here: 104 us
  Pallas kernels  102 us (97%)
  local copies, waits for them, and re-layouts  1.88 us (2%)
    pallas_call x1, Pallas kernels, local(): pl.pallas_call(body, out_shape=jax.ShapeDtypeStruct((1, tokens, piece), b...  102 us

profile of v3, /device:TPU:29, one launch (start us, length us, event | category | flops | bytes accessed | tf_op | source)
XLA Modules:
  0.0 104.4 jit_solution(13837584276023631667)
XLA Ops:
  0.7 101.8 %shard_map.91 = bf16[1,128,2048]{2,1,0:T(8,128)(2,1)} custom-call(bf16[128,4096]{1,0:T(8,128)(2,1)} %hidden.1, s32[4,32]{1,0:T(4,128)} %ids.1, s32[4,8]{1,0:T(4,128)} %seg_job.1, s32[6]{0:T(128)} %job_ad.1, s32[1]{0:T(128)S(6)} %copy.11.owner, bf16[1,8192,2048]{2,1,0:T(8,128)(2,1)} %frozen.1, bf16[1,4096]{1,0:T(2,128)(2,1)} %gain.1, ...), custom_call_target="tpu_custom_call" | custom-call | tf_op jit(solution)/shard_map/pallas_call | solution.py:652
  102.5 1.9 %copy.12 = bf16[1,128,2048]{2,1,0:T(8,128)(2,1)} copy(bf16[1,128,2048]{2,1,0:T(8,128)(2,1)} %shard_map.91) | data formatting | bytes 1048576

commit v4 on v3

--- a/solution.py
+++ b/solution.py
@@ -9,7 +9,7 @@
 R = 32
 TILE = 256
 UNIT = 32
-DIRECT = 0
+WIDE = False
 EARLY = 0
 DELAYS = (0, 4, 8, 12)
 TAIL = 1
@@ -69,7 +69,6 @@
     tiles = piece // TILE
     segs, jobs = jobs_of
     window = 6
-    direct = min(DIRECT, chunks - 1)
     early = min(EARLY, chunks - 1)
     s = lax.axis_index("section")
     t = lax.axis_index("tensor")
@@ -134,12 +133,10 @@
     @pl.when(level > 0)
     def _():
         greet(s - 2, t)
-        greet(other - 2, t)
 
     @pl.when(level < levels - 1)
     def _():
         greet(s + 2, t)
-        greet(other + 2, t)
 
     @pl.when(level == 0)
     def _():
@@ -204,7 +201,7 @@
 
     ends = (level > 0).astype(jnp.int32) + (level < levels - 1).astype(jnp.int32)
     with jax.named_scope("barrier"):
-        pl.semaphore_wait(barrier, 2 * tensors - 1 + 2 * ends)
+        pl.semaphore_wait(barrier, 2 * tensors - 1 + ends)
 
     def send_hidden(d):
         return remote(x0.at[t], x0.at[t], hidsend.at[d], hidsem.at[t], s, peer(d))
@@ -229,28 +226,23 @@
         read_up(d).wait()
         send_up(d).start()
 
-    def send_out(m, c):
-        return remote(outbuf.at[m, c], xbuf.at[m, b, c], osend.at[m], ysem.at[m, c], s + 2, t)
-
-    def send_across(m, c):
-        return remote(outbuf.at[m, c], xbuf.at[m, b, c], osend.at[m], xsem.at[m, c], other + 2, t)
-
-    def send_both(m, c):
-        send_out(m, c).start()
-        if c >= chunks - direct:
-            send_across(m, c).start()
+    def send_out(m, c, i):
+        return remote(outbuf.at[m, c, i], xbuf.at[m, b, c, i], osend.at[m], ysem.at[m, c, i], s + 2, t)
+
+    def send_next(m, c):
+        for i in range(inner):
+            send_out(m, c, i).start()
 
     def sent(m):
         landed(outbuf.at[m], osend.at[m])
-        if direct:
-            landed(outbuf.at[m, 0:direct], osend.at[m])
 
     def write_out(m, c):
         def write(size):
             here = pl.ds(pl.multiple_of(m * rows, 8), size)
-            pltpu.make_async_copy(
-                outbuf.at[m, c, 0:size], out.at[0, here, at(c * step, step)], wout.at[m]
-            ).start()
+            for i in range(inner):
+                pltpu.make_async_copy(
+                    outbuf.at[m, c, i, 0:size], out.at[0, here, at(c * step + i * TILE, TILE)], wout.at[m]
+                ).start()
 
         if short == rows:
             write(rows)
@@ -368,14 +360,13 @@
                 fresh = old + pltpu.matmul_pop(accs[j][q]) * scale
                 for m in range(units):
                     size = short if m == units - 1 else rows
-                    cols = slice(q * TILE, (q + 1) * TILE)
-                    outbuf[m, j, 0:size, cols] = fresh[m * rows : m * rows + size].astype(bf16)
+                    outbuf[m, j, q, 0:size] = fresh[m * rows : m * rows + size].astype(bf16)
                     if size < rows:
-                        outbuf[m, j, size:, cols] = jnp.zeros((rows - size, TILE), bf16)
+                        outbuf[m, j, q, size:] = jnp.zeros((rows - size, TILE), bf16)
 
             @pl.when(jnp.logical_not(last))
             def _():
-                send_both(0, j)
+                send_next(0, j)
             for m in range(units):
                 write_out(m, j)
 
@@ -400,11 +391,11 @@
             for m in range(1, units):
                 sent(m - 1)
                 for j in range(chunks):
-                    send_both(m, j)
+                    send_next(m, j)
             sent(units - 1)
 
     arrivals = sorted((c + delay, kind, c) for kind, delay in enumerate(DELAYS) for c in range(chunks))
-    lead = min(3, inner * chunks - 1)
+    lead = min(1, inner * chunks - 1)
 
     def label(name, step):
         step.label = name
@@ -428,18 +419,18 @@
         work = [(kind, c) + p for _, kind, c in arrivals for p in pieces(kind)]
 
         def arrive(m, kind, c, owner_of, blk):
-            ref = xbuf.at[m, blk, c]
-            if kind == 0:
-                landed(ref, ysem.at[m, c])
-                if c < chunks - direct:
-                    remote(ref, ref, xsend.at[m], xsem.at[m, c], other, t).start()
-            elif kind == 2:
-                landed(ref, xsem.at[m, c])
-            else:
-                landed(ref, psem.at[m, owner_of, kind // 2, c])
-            if kind % 2 == 0:
-                for d in range(1, tensors):
-                    remote(ref, ref, fsend.at[m], psem.at[m, t, kind // 2, c], s, peer(d)).start()
+            for i in range(inner):
+                ref = xbuf.at[m, blk, c, i]
+                if kind == 0:
+                    landed(ref, ysem.at[m, c, i])
+                    remote(ref, ref, xsend.at[m], xsem.at[m, c, i], other, t).start()
+                elif kind == 2:
+                    landed(ref, xsem.at[m, c, i])
+                else:
+                    landed(ref, psem.at[m, owner_of, kind // 2, c, i])
+                if kind % 2 == 0:
+                    for d in range(1, tensors):
+                        remote(ref, ref, fsend.at[m], psem.at[m, t, kind // 2, c, i], s, peer(d)).start()
 
         def unit_steps(m):
             here = {"square": jnp.zeros((rows, 128), f32)}
@@ -447,14 +438,17 @@
 
             def prepare(key):
                 _, c, owner_of, blk, gains = work[key]
-                x = xbuf[m, blk, c].astype(f32)
-                here[key] = x * gains[0:1, at(owner_of * piece + c * step, step)].astype(f32)
-                for v in range(step // 128):
-                    y = x[:, v * 128 : (v + 1) * 128]
-                    here["square"] = here["square"] + y * y
+                here[key] = []
+                for i in range(inner):
+                    x = xbuf[m, blk, c, i].astype(f32)
+                    g = gains[0:1, at(owner_of * piece + c * step + i * TILE, TILE)].astype(f32)
+                    here[key].append((x * g).astype(bf16) if WIDE else x * g)
+                    for v in range(TILE // 128):
+                        y = x[:, v * 128 : (v + 1) * 128]
+                        here["square"] = here["square"] + y * y
 
             def lhs(key, i):
-                return lambda: here[key][:, i * TILE : (i + 1) * TILE]
+                return lambda: here[key][i]
 
             def product(key, i, j):
                 _, c, _, blk, _ = work[key]
@@ -508,14 +502,13 @@
 
             def leave(j):
                 for q in range(2):
-                    cols = slice(q * TILE, (q + 1) * TILE)
-                    old = xbuf[m, b, j, :, cols].astype(f32)
+                    old = xbuf[m, b, j, q].astype(f32)
                     fresh = old + pltpu.matmul_pop(accs[j][q]) * here["scale"]
-                    outbuf[m, j, :, cols] = fresh.astype(bf16)
+                    outbuf[m, j, q] = fresh.astype(bf16)
 
                 @pl.when(jnp.logical_not(last))
                 def _():
-                    send_both(m, j)
+                    send_next(m, j)
                 write_out(m, j)
                 if j < early:
                     @pl.when(m + 1 < units)
@@ -586,8 +579,7 @@
                 pltpu.matmul_pop(accs[0][q])
 
         for m in range(units):
-            if chunks > direct:
-                landed(xbuf.at[m, 0, 0 : chunks - direct], xsend.at[m])
+            landed(xbuf.at[m, 0], xsend.at[m])
             if tensors > 1:
                 landed(xbuf.at[m, 0 : 2 * (tensors - 1)], fsend.at[m])
             landed(lowbuf.at[0 : 2 * tensors - 1, m * rows : (m + 1) * rows], lsend.at[m])
@@ -625,7 +617,7 @@
             sent(m)
 
     for m in range(units):
-        landed(outbuf.at[m, :, 0 : short if m == units - 1 else rows], wout.at[m])
+        landed(outbuf.at[m, :, :, 0 : short if m == units - 1 else rows], wout.at[m])
 
 
 def local(
@@ -638,6 +630,7 @@
     ranks = inbox_down.shape[3]
     step = 2 * TILE
     chunks = piece // step
+    inner = step // TILE
     tokens = batches[0] * batches[1]
     rows = min(UNIT, tokens)
     units = -(-tokens // rows)
@@ -658,8 +651,8 @@
             pltpu.VMEM((depth, piece), bf16),
             pltpu.VMEM((tensors, tokens, 2 * piece), bf16),
             pltpu.VMEM((depth // TILE, tokens, TILE), bf16),
-            pltpu.VMEM((units, 2 * tensors, chunks, rows, step), bf16),
-            pltpu.VMEM((units, chunks, rows, step), bf16),
+            pltpu.VMEM((units, 2 * tensors, chunks, inner, rows, TILE), bf16),
+            pltpu.VMEM((units, chunks, inner, rows, TILE), bf16),
             pltpu.VMEM(norm_gain.shape, bf16),
             pltpu.VMEM((tensors, piece, ranks), bf16),
             pltpu.VMEM((tensors, ranks, piece), bf16),
@@ -679,9 +672,9 @@
             dma((tensors,)),
             dma((2, tensors)),
             dma((2,)),
-            dma((units, chunks)),
-            dma((units, chunks)),
-            dma((units, tensors, 2, chunks)),
+            dma((units, chunks, inner)),
+            dma((units, chunks, inner)),
+            dma((units, tensors, 2, chunks, inner)),
             dma((units, 2 * tensors)),
             dma((units,)),
             dma((units,)),

time: 105 us -> 103 us (0.981)
  Pallas kernels: 102 us -> 100 us
    pallas_call x1, Pallas kernels: 102 us -> 100 us  [local(): pl.pallas_call(body, out_shape=jax.ShapeDtypeStruct((1, tokens, piece), b...]
where the time goes in v4:
time: 103 us
  Pallas kernels  100 us (97%)
  local copies, waits for them, and re-layouts  1.88 us (2%)
    pallas_call x1, Pallas kernels, local(): pl.pallas_call(body, out_shape=jax.ShapeDtypeStruct((1, tokens, piece), b...  100 us

profile of v4, /device:TPU:29, one launch (start us, length us, event | category | flops | bytes accessed | tf_op | source)
XLA Modules:
  0.0 102.9 jit_solution(4084405170533509298)
XLA Ops:
  0.7 100.3 %shard_map.91 = bf16[1,128,2048]{2,1,0:T(8,128)(2,1)} custom-call(bf16[128,4096]{1,0:T(8,128)(2,1)} %hidden.1, s32[4,32]{1,0:T(4,128)} %ids.1, s32[4,8]{1,0:T(4,128)} %seg_job.1, s32[6]{0:T(128)} %job_ad.1, s32[1]{0:T(128)S(6)} %copy.11.owner, bf16[1,8192,2048]{2,1,0:T(8,128)(2,1)} %frozen.1, bf16[1,4096]{1,0:T(2,128)(2,1)} %gain.1, ...), custom_call_target="tpu_custom_call" | custom-call | tf_op jit(solution)/shard_map/pallas_call | solution.py:645
  101.0 1.9 %copy.12 = bf16[1,128,2048]{2,1,0:T(8,128)(2,1)} copy(bf16[1,128,2048]{2,1,0:T(8,128)(2,1)} %shard_map.91) | data formatting | bytes 1048576
